TPU v7x, 128 devices: a whole 4x4x4 slice. The times are simulated.
128 devices in a mesh: grp: 4 (over z), dev: 32 (over x, y, core).
Axes of the slice: x: 4, y: 4, z: 4, core: 2. Of those that a mesh axis runs over, the one named last changes fastest.
Arguments:
- inv_factor: bfloat16 [512, 384, 384], P(('grp', 'dev')), may hold values from -8 to 8
- border: bfloat16 [512, 384, 2048], P(('grp', 'dev')), may hold values from -0.107910156 to 0.107910156
- block_rows: int32 [512], P(('grp', 'dev')), may hold values from 96 to 384
- live_count: int32 [128], P(('grp', 'dev')), may hold values from 1 to 4, as said below
- first_section: float32 [2048, 2048], P('dev'), may hold values from -6 to 6
Outputs:
- condensed: bfloat16 [512, 384, 2048], P(('grp', 'dev'))
- schur: float32 [2048, 2048], P('dev')
Inputs may be any that keep to these rules, and one draw needn't show every extreme that they name: `live_count`: every device holds 1 to 4 live scenarios; at least one device holds 4.
All inputs are finite; a program needn't handle non-finite values.
Results may differ from a plain program's by a relative error of at most 0.001.
Values sent between devices are 32-bit elements; how exact they have to be, the bound alone decides.
A program may use at most 192 MiB of HBM per device.

v0:
```python
import jax
import jax.numpy as jnp
from jax import lax
from jax.sharding import PartitionSpec as P


def from_everyone(value, axis):
    devices = lax.axis_size(axis)
    return lax.all_to_all(
        jnp.broadcast_to(value[None], (devices, *value.shape)), axis, 0, 0, tiled=True
    )


def taken_together(value, axis):
    everything = from_everyone(value, axis)
    return jnp.sum(everything, axis=0)


def condense(inverse, border_piece):
    return jnp.dot(inverse, border_piece, preferred_element_type=jnp.float32).astype(jnp.bfloat16)


def fill_slots(buffer, source_inv, source_border, start_slot, number):

    def fill_one_step(step, current):
        inverse = lax.dynamic_index_in_dim(source_inv, start_slot + step, 0, keepdims=False)
        border_piece = lax.dynamic_index_in_dim(source_border, start_slot + step, 0, keepdims=False)
        return lax.dynamic_update_index_in_dim(
            current, condense(inverse, border_piece), start_slot + step, 0
        )

    return lax.fori_loop(0, number, fill_one_step, buffer)


def accumulate(buffer, number, term_fn, out_shape):

    def accumulate_one_step(step, current):
        piece = lax.dynamic_index_in_dim(buffer, step, 0, keepdims=False)
        return current + term_fn(piece)

    return lax.fori_loop(0, number, accumulate_one_step, jnp.zeros(out_shape, jnp.float32))


def column_product(columns, piece):
    return lax.dot_general(
        columns, piece, (((0,), (0,)), ((), ())), preferred_element_type=jnp.float32
    )


def body(inv_factor, border, block_rows, live_count, first_section):
    slots, rows_block, width = border.shape
    count_own = live_count[0]
    row_ids = lax.broadcasted_iota(jnp.int32, (slots, rows_block, 1), 1)
    masked_inv = jnp.where(
        row_ids < block_rows[:, None, None], inv_factor, jnp.zeros_like(inv_factor)
    )
    empty = jnp.zeros(border.shape, jnp.bfloat16)
    condensed = fill_slots(empty, masked_inv, border, 0, count_own)
    rows_dev = width // lax.axis_size("dev")
    share = lax.psum_scatter(
        accumulate(
            condensed,
            count_own,
            lambda piece: column_product(piece, piece),
            (lax.axis_size("dev") * rows_dev, width),
        ),
        "dev",
        scatter_dimension=0,
        tiled=True,
    )
    summed = taken_together(share, "grp")
    return (condensed, first_section - summed)


def solution(mesh):
    placed = (
        P(("grp", "dev"), None, None),
        P(("grp", "dev"), None, None),
        P(("grp", "dev")),
        P(("grp", "dev")),
        P("dev", None),
    )
    return jax.shard_map(
        body,
        mesh=mesh,
        in_specs=placed,
        out_specs=(P(("grp", "dev"), None, None), P("dev", None)),
        check_vma=False,
    )
```

profile of v0, /device:TPU:1, one launch (start us, length us, event | category | flops | bytes accessed | tf_op | source)
XLA Modules:
  0.0 263.5 jit_solution(3813958559946132322)
XLA Ops:
  7.2 0.0 reduce-scatter.2.cloned.1.call-start
  7.2 0.7 iota_compare_fusion
  7.9 1.5 broadcast_select_fusion
  9.5 3.5 %broadcast_in_dim.28 = bf16[4,384,2048]{2,1,0:T(8,128)(2,1)} broadcast(bf16[]{:T(256)} %constant.30.clone.1), dimensions={} | broadcast | bytes 6291458 | tf_op jit(solution)/shard_map/broadcast_in_dim | solution.py:57
  13.0 4.8 %while.20 = (s32[]{:T(128)}, bf16[4,384,2048]{2,1,0:T(8,128)(2,1)}, s32[]{:T(128)}, bf16[4,384,384]{2,1,0:T(8,128)(2,1)S(1)}, bf16[4,384,2048]{2,1,0:T(8,128)(2,1)}, /*index=5*/s32[]{:T(128)}, s32[]{:T(128)}, s32[]{:T(128)}) while((s32[]{:T(128)}, bf16[4,384,2048]{2,1,0:T(8,128)(2,1)}, s32[]{:T(128)}, bf16[4,384,384]{2,1,0:T(8,128)(2,1)S(1)}, ...), condition=%wide.region_1.2_spmd, body=%wide.region_0.1_spmd.sunk | while | flops 604766208 | bytes 3442303 | solution.py:32
  13.7 3.5 %fusion.16 = bf16[4,384,2048]{2,1,0:T(8,128)(2,1)} fusion(bf16[4,384,2048]{2,1,0:T(8,128)(2,1)} %get-tuple-element.140, s32[]{:T(128)S(6)} %select_n.20, bf16[4,384,2048]{2,1,0:T(8,128)(2,1)} %get-tuple-element.151, bf16[4,384,384]{2,1,0:T(8,128)(2,1)S(1)} %get-tuple-element.150), kind=kOutput, calls=%fused_computation.2.clone.1 | convolution fusion | flops 604766208 | bytes 3442176 | tf_op jit(solution)/shard_map/while/body/dot_general | solution.py:20
  17.8 7.8 %broadcast_in_dim.31 = f32[2048,2048]{1,0:T(8,128)} broadcast(f32[]{:T(128)} %constant.31.clone.1), dimensions={} | broadcast | bytes 16777220 | tf_op jit(solution)/shard_map/broadcast_in_dim | solution.py:41
  25.7 18.3 %while.21 = (s32[]{:T(128)}, f32[2048,2048]{1,0:T(8,128)}, s32[]{:T(128)}, bf16[4,384,2048]{2,1,0:T(8,128)(2,1)}, s32[]{:T(128)}, /*index=5*/s32[]{:T(128)}, s32[]{:T(128)}) while((s32[]{:T(128)}, f32[2048,2048]{1,0:T(8,128)}, s32[]{:T(128)}, bf16[4,384,2048]{2,1,0:T(8,128)(2,1)}, s32[]{:T(128)}, /*index=5*/s32[]{:T(128)}, s32[]{:T(128)}) %tuple.38), condition=%wide.region_3.4_spmd, body=%wide.region_2.3_spmd.sunk | while | flops 3225419776 | bytes 35127416 | solution.py:41
  26.4 17.0 %convolution_add_fusion.2 = f32[2048,2048]{1,0:T(8,128)} fusion(f32[2048,2048]{1,0:T(8,128)} %get-tuple-element.163, bf16[4,384,2048]{2,1,0:T(8,128)(2,1)} %get-tuple-element.172, s32[]{:T(128)S(6)} %select_n.21), kind=kOutput, calls=%fused_computation.8.clone.1 | convolution fusion | flops 3225419776 | bytes 35127300 | tf_op jit(solution)/shard_map/while/body/dot_general | solution.py:45
  44.0 0.0 reduce-scatter.2.cloned.1.call-update
  44.1 0.0 copy-start
  44.1 182.4 %reduce-scatter.2.cloned.1.call-done = f32[64,2048]{1,0:T(8,128)} async-done(((f32[2048,2048]{1,0:T(8,128)}), f32[64,2048]{1,0:T(8,128)}) %reduce-scatter.2.cloned.1.call-update) | async-done | bytes 524304 | tf_op jit(solution)/shard_map/reduce_scatter | solution.py:60
  226.5 1.3 broadcast_in_dim.32
  227.7 27.9 %all_to_all.5 = f32[4,64,2048]{2,1,0:T(8,128)S(1)} all-to-all(f32[4,64,2048]{2,1,0:T(8,128)S(1)} %broadcast_in_dim.32), channel_id=1, replica_groups=mesh['grp'=4,'dev'=32] {'grp'}, dimensions={0} | all-to-all | bytes 4194304 | tf_op jit(solution)/shard_map/all_to_all | solution.py:9
  255.7 0.2 reduce_sum.9
  255.8 0.0 copy-done
  255.8 0.9 sub.3
Async XLA Ops:
  7.2 219.3 %reduce-scatter.2.cloned.1.call-start = ((), (), s32[]{:S(2)}) async-start(), calls=%async_computation.2 | async-start | bytes 17301504 | tf_op jit(solution)/shard_map/reduce_scatter | solution.py:60
  44.1 211.8 %copy-start = (f32[64,2048]{1,0:T(8,128)S(1)}, f32[64,2048]{1,0:T(8,128)}, u32[]{:S(2)}) copy-start(f32[64,2048]{1,0:T(8,128)} %param.13) | copy-start | bytes 1572868
Sparse Core Ops, SparseCore 0:
  44.2 182.2 reduce-scatter.1
where the time goes:
time: 266 us; the launch traced here: 264 us
  waiting for transfers between devices  182 us (68%)
  blocking collectives  27.9 us (10%)
  matrix products  20.6 us (8%)
  between operations  14.1 us (5%)
  local copies, waits for them, and re-layouts  12.6 us (5%)
  other arithmetic  3.28 us (1%)
    reduce_scatter x1, waiting for transfers between devices, body(): lax.psum_scatter(accumulate(condensed, count_own, lambda piece: column_pr...  182 us
    all_to_all x1, blocking collectives, from_everyone(): lax.all_to_all(jnp.broadcast_to(value[None], (devices, *value.shape)), ax...  27.9 us
    dot_general x1, matrix products, column_product(): lax.dot_general(columns, piece, (((0,), (0,)), ((), ())), preferred_eleme...  17 us
    broadcast_in_dim x1, local copies, waits for them, and re-layouts, accumulate(): jnp.zeros(out_shape, jnp.float32)  7.85 us
  transfers between devices with their start and end apart: 1, of which 1 were waited for; matrix products, arithmetic and copies ran while one was open for 0% of the time, Pallas kernels for 0%

commit v1 on v0

v1 whole, which is shorter than its diff:
```python
import functools

import jax
import jax.numpy as jnp
from jax import lax
from jax.experimental import pallas as pl
from jax.experimental.pallas import tpu as pltpu
from jax.sharding import PartitionSpec as P

MESH = pl.DeviceIdType.MESH
SIDE = 4
BLK = 128
PIECE = BLK // 2 // SIDE
WIDE = 384
PARTS = 3


def condense_kernel(live_ref, rows_ref, inv_ref, border_ref, out_ref):
    slot = pl.program_id(0)
    rows = jnp.where(slot < live_ref[0], rows_ref[slot], 0)
    inverse = inv_ref[0]
    ids = lax.broadcasted_iota(jnp.int32, inverse.shape, 0)
    masked = jnp.where(ids < rows, inverse, jnp.zeros_like(inverse))
    out_ref[0] = jnp.dot(masked, border_ref[0], preferred_element_type=jnp.float32).astype(out_ref.dtype)


def condense(live_count, block_rows, inv_factor, border):
    slots, order, width = border.shape
    tile = width // 2
    return pl.pallas_call(
        condense_kernel,
        grid_spec=pltpu.PrefetchScalarGridSpec(
            num_scalar_prefetch=2,
            grid=(slots, width // tile),
            in_specs=[
                pl.BlockSpec((1, order, order), lambda s, j, *_: (s, 0, 0)),
                pl.BlockSpec((1, order, tile), lambda s, j, *_: (s, 0, j)),
            ],
            out_specs=pl.BlockSpec((1, order, tile), lambda s, j, *_: (s, 0, j)),
        ),
        out_shape=jax.ShapeDtypeStruct(border.shape, border.dtype),
        name="condense",
    )(live_count, block_rows, inv_factor, border)


def assemble_kernel(
    cond_ref, first_ref, out_ref,
    c_buf, ct_buf, g_buf, r_buf,
    rel0, rel1, rel2, left0, left1, left2, right0, right1, right2,
    q_buf, q_rel, q_left, q_right, w_buf, w_rel, w_left, w_right,
    z_buf, x_buf, t_buf, e_buf,
    load_sem, send_sem, recv_sem, e_sem,
):
    dev = lax.axis_index("dev")
    z = lax.axis_index("grp")
    core = dev % 2
    pair = dev // 2
    x, y = pair // SIDE, pair % SIDE
    other = 1 - core

    def at(xx, yy, zz, cc):
        return (zz, (xx * SIDE + yy) * 2 + cc)

    def near(axis, step):
        s = SIDE + step
        if axis == "x":
            return at((x + s) % SIDE, y, z, core)
        if axis == "y":
            return at(x, (y + s) % SIDE, z, core)
        return at(x, y, (z + s) % SIDE, core)

    sent = []

    def remote(src, dst, target, arrival=None):
        n = len(sent)
        copy = pltpu.make_async_remote_copy(
            src_ref=src, dst_ref=dst, send_sem=send_sem.at[n],
            recv_sem=recv_sem.at[n] if arrival is None else arrival,
            device_id=target, device_id_type=MESH,
        )
        sent.append(copy)
        copy.start()
        return copy

    order_x = (0, 1, 2, 3)
    order_y = ((y + 2) % SIDE, (y + 1) % SIDE, (y + 3) % SIDE, y)
    order_z = ((z + 2) % SIDE, (z + 1) % SIDE, (z + 3) % SIDE, z)

    barrier = pltpu.get_barrier_semaphore()
    peers = [at(x, y, z, other), near("z", 1), near("z", -1)]
    for r in range(1, 2 * SIDE):
        for turn in (r, 4 * SIDE - r):
            peer = (pair + turn) % (SIDE * SIDE)
            for cc in range(2):
                peers.append((z, peer * 2 + cc))
    for peer in peers:
        pl.semaphore_signal(barrier, inc=1, device_id=peer, device_id_type=MESH)

    tiles = c_buf.shape[2] // (2 * BLK)
    first_tile = (2 * ((x + 2) % SIDE)) % tiles
    loads = []
    for n in range(tiles):
        cols = pl.ds(pl.multiple_of(((first_tile + n) % tiles) * 2 * BLK, 2 * BLK), 2 * BLK)
        copy = pltpu.make_async_copy(cond_ref.at[:, :, cols], c_buf.at[:, :, cols], load_sem.at[n])
        copy.start()
        loads.append(copy)

    depth = c_buf.shape[0] * c_buf.shape[1]

    def tile_of(n):
        cols = pl.ds(pl.multiple_of((n % tiles) * 2 * BLK, 2 * BLK), 2 * BLK)
        return c_buf[:, :, cols].reshape(depth, 2 * BLK)

    def gram(h, yh):
        xx = (x + (2, 1, 3, 0)[h]) % SIDE
        i = 2 * xx + yh
        ct_buf[...] = jnp.transpose(tile_of(i))
        for j in range(5):
            product = jnp.dot(ct_buf[...], tile_of(i + j), preferred_element_type=jnp.float32)
            for a in range(2):
                for b in range(2):
                    rel = 2 * j + b - a
                    if 0 <= rel <= 8:
                        block = product[a * BLK:(a + 1) * BLK, b * BLK:(b + 1) * BLK]
                        off = BLK * (rel % 3)
                        g_buf[:, h, rel // 3, 2 * yh + a, :, :, off:off + BLK] = block.reshape(2, SIDE, PIECE, BLK)

    mine = g_buf.at[core]
    swaps = {}
    stage = {}

    def swap(h, yh):
        half = pl.ds(2 * yh, 2)
        swaps[h, yh] = remote(g_buf.at[other, h, :, half], r_buf.at[h, yh], at(x, y, z, other))

    def join(h, yh):
        swaps[h, yh].wait_recv()
        half = pl.ds(2 * yh, 2)
        for k in range(PARTS):
            g_buf[core, h, k, half] = g_buf[core, h, k, half] + r_buf[h, yh, k]

    lo, hi = pl.ds(0, 2), pl.ds(2, 2)

    def launch(h):
        yo, yr, yl, _ = order_y
        zo, zr, zl, _ = order_z
        if h == 0:
            stage["r0"] = remote(mine.at[0, 0, lo], rel0.at[0], near("x", 1))
            stage["l0"] = remote(mine.at[0, 0, hi], rel0.at[1], near("x", -1))
        stage["r1", h] = remote(mine.at[h, 1, yo, lo], rel1.at[h, 0], near("y", 1))
        stage["l1", h] = remote(mine.at[h, 1, yo, hi], rel1.at[h, 1], near("y", -1))
        stage["r2", h] = remote(mine.at[h, 2, lo, zo], rel2.at[h, 0], near("z", 1))
        stage["l2", h] = remote(mine.at[h, 2, hi, zo], rel2.at[h, 1], near("z", -1))
        if h == 1:
            stage["p0r"] = remote(mine.at[1, 0, hi], left0.at[hi], near("x", 1))
        if h == 2:
            stage["p0l"] = remote(mine.at[2, 0, lo], right0.at[lo], near("x", -1))
        stage["p1r", h] = remote(mine.at[h, 1, yr, hi], left1.at[h, hi], near("y", 1))
        stage["p1l", h] = remote(mine.at[h, 1, yl, lo], right1.at[h, lo], near("y", -1))
        stage["p2r", h] = remote(mine.at[h, 2, hi, zr], left2.at[h, hi], near("z", 1))
        stage["p2l", h] = remote(mine.at[h, 2, lo, zl], right2.at[h, lo], near("z", -1))

    def pass_x(h):
        if h == 1:
            stage["r0"].wait_recv()
            g_buf[core, 1, 0, lo] = g_buf[core, 1, 0, lo] + rel0[0]
            stage["f0r"] = remote(mine.at[1, 0, lo], left0.at[lo], near("x", 1))
        if h == 2:
            stage["l0"].wait_recv()
            g_buf[core, 2, 0, hi] = g_buf[core, 2, 0, hi] + rel0[1]
            stage["f0l"] = remote(mine.at[2, 0, hi], right0.at[hi], near("x", -1))

    def pass_yz(h):
        _, yr, yl, _ = order_y
        _, zr, zl, _ = order_z
        stage["r1", h].wait_recv()
        g_buf[core, h, 1, yr, lo] = g_buf[core, h, 1, yr, lo] + rel1[h, 0]
        stage["f1r", h] = remote(mine.at[h, 1, yr, lo], left1.at[h, lo], near("y", 1))
        stage["l1", h].wait_recv()
        g_buf[core, h, 1, yl, hi] = g_buf[core, h, 1, yl, hi] + rel1[h, 1]
        stage["f1l", h] = remote(mine.at[h, 1, yl, hi], right1.at[h, hi], near("y", -1))
        stage["r2", h].wait_recv()
        g_buf[core, h, 2, lo, zr] = g_buf[core, h, 2, lo, zr] + rel2[h, 0]
        stage["f2r", h] = remote(mine.at[h, 2, lo, zr], left2.at[h, lo], near("z", 1))
        stage["l2", h].wait_recv()
        g_buf[core, h, 2, hi, zl] = g_buf[core, h, 2, hi, zl] + rel2[h, 1]
        stage["f2l", h] = remote(mine.at[h, 2, hi, zl], right2.at[h, hi], near("z", -1))

    for s in range(8):
        if s == 0:
            for copy in loads[:5]:
                copy.wait()
        elif s == 1:
            loads[5].wait()
        elif s == 2:
            for copy in loads[6:]:
                copy.wait()
        gram(s // 2, s % 2)
        if s == 0:
            pl.semaphore_wait(barrier, len(peers))
        swap(s // 2, s % 2)
        if s >= 1:
            join((s - 1) // 2, (s - 1) % 2)
            if s % 2 == 0:
                h = s // 2 - 1
                launch(h)
                pass_x(h)
                if h >= 1:
                    pass_yz(h - 1)
    join(3, 1)
    launch(3)
    pass_yz(2)
    pass_yz(3)

    for name in ("p0r", "f0r", "p0l", "f0l"):
        stage[name].wait_recv()
    for yy in range(SIDE):
        q_buf[0, yy] = g_buf[core, 3, 0, yy] + left0[yy] + right0[yy]
    for h in range(SIDE):
        for name in ("p1r", "f1r", "p1l", "f1l"):
            stage[name, h].wait_recv()
        for zz in range(SIDE):
            q_buf[1, zz, h] = g_buf[core, h, 1, y, zz] + left1[h, zz] + right1[h, zz]
    for h in range(SIDE):
        for name in ("p2r", "f2r", "p2l", "f2l"):
            stage[name, h].wait_recv()
        for yy in range(SIDE):
            q_buf[2, h, yy] = g_buf[core, h, 2, yy, z] + left2[h, yy] + right2[h, yy]

    axes2 = (("y", order_y), ("z", order_z), ("x", order_x))
    hops = {}
    for k, (axis, (opp, rgt, lft, own)) in enumerate(axes2):
        hops["r", k] = remote(q_buf.at[k, opp, lo], q_rel.at[k, 0], near(axis, 1))
        hops["l", k] = remote(q_buf.at[k, opp, hi], q_rel.at[k, 1], near(axis, -1))
    for k, (axis, (opp, rgt, lft, own)) in enumerate(axes2):
        hops["pr", k] = remote(q_buf.at[k, rgt, hi], q_left.at[k, hi], near(axis, 1))
        hops["pl", k] = remote(q_buf.at[k, lft, lo], q_right.at[k, lo], near(axis, -1))
    for k, (axis, (opp, rgt, lft, own)) in enumerate(axes2):
        hops["r", k].wait_recv()
        q_buf[k, rgt, lo] = q_buf[k, rgt, lo] + q_rel[k, 0]
        hops["fr", k] = remote(q_buf.at[k, rgt, lo], q_left.at[k, lo], near(axis, 1))
        hops["l", k].wait_recv()
        q_buf[k, lft, hi] = q_buf[k, lft, hi] + q_rel[k, 1]
        hops["fl", k] = remote(q_buf.at[k, lft, hi], q_right.at[k, hi], near(axis, -1))
    for k, (axis, (opp, rgt, lft, own)) in enumerate(axes2):
        for name in ("pr", "fr", "pl", "fl"):
            hops[name, k].wait_recv()
        w_buf[k] = q_buf[k, own] + q_left[k] + q_right[k]

    top, low = pl.ds(0, PIECE // 2), pl.ds(PIECE // 2, PIECE // 2)
    axes3 = (("z", order_z), ("x", order_x), ("y", order_y))
    hops = {}
    for k, (axis, (opp, rgt, lft, own)) in enumerate(axes3):
        hops["r", k] = remote(w_buf.at[k, opp, top], w_rel.at[k, 0], near(axis, 1))
        hops["l", k] = remote(w_buf.at[k, opp, low], w_rel.at[k, 1], near(axis, -1))
    for k, (axis, (opp, rgt, lft, own)) in enumerate(axes3):
        hops["pr", k] = remote(w_buf.at[k, rgt, low], w_left.at[k, low], near(axis, 1))
        hops["pl", k] = remote(w_buf.at[k, lft, top], w_right.at[k, top], near(axis, -1))
    for k, (axis, (opp, rgt, lft, own)) in enumerate(axes3):
        hops["r", k].wait_recv()
        w_buf[k, rgt, top] = w_buf[k, rgt, top] + w_rel[k, 0]
        hops["fr", k] = remote(w_buf.at[k, rgt, top], w_left.at[k, top], near(axis, 1))
        hops["l", k].wait_recv()
        w_buf[k, lft, low] = w_buf[k, lft, low] + w_rel[k, 1]
        hops["fl", k] = remote(w_buf.at[k, lft, low], w_right.at[k, low], near(axis, -1))
    for k, (axis, (opp, rgt, lft, own)) in enumerate(axes3):
        for name in ("pr", "fr", "pl", "fl"):
            hops[name, k].wait_recv()
        z_buf[0, k] = w_buf[k, own] + w_left[k] + w_right[k]

    ra = remote(z_buf.at[0, :, top], z_buf.at[1, :, top], near("z", 1))
    lb = remote(z_buf.at[0, :, low], z_buf.at[2, :, low], near("z", -1))
    rb = remote(z_buf.at[0, :, low], z_buf.at[1, :, low], near("z", 1))
    la = remote(z_buf.at[0, :, top], z_buf.at[2, :, top], near("z", -1))
    ra.wait_recv()
    fa = remote(z_buf.at[1, :, top], z_buf.at[3, :, top], near("z", 1))
    lb.wait_recv()
    fb = remote(z_buf.at[2, :, low], z_buf.at[3, :, low], near("z", -1))
    for copy in (rb, la, fa, fb):
        copy.wait_recv()
    for slot, turn in enumerate((0, 3, 1, 2)):
        rows = pl.ds(pl.multiple_of(((z + turn) % SIDE) * PIECE, PIECE), PIECE)
        for k in range(PARTS):
            x_buf[rows, k * WIDE:(k + 1) * WIDE] = z_buf[slot, k]

    for r in range(1, 2 * SIDE):
        block = x_buf[:, r * BLK:(r + 1) * BLK]
        both = jnp.concatenate([block, pltpu.roll(block, BLK - 32, 1)], axis=0)
        turned = jnp.transpose(both)
        peer = (pair + r) % (SIDE * SIDE)
        for cc in range(2):
            t_buf[r - 1, cc] = turned[64 * cc:64 * cc + 32]
        for cc in range(2):
            remote(t_buf.at[r - 1, cc], e_buf.at[r - 1, core], (z, peer * 2 + cc), e_sem.at[r - 1, core])
    for rel in range(9):
        cols = pl.ds(pl.multiple_of(((pair + rel) % (SIDE * SIDE)) * BLK, BLK), BLK)
        out_ref[:, cols] = first_ref[:, cols] - x_buf[:, rel * BLK:(rel + 1) * BLK]
    lane = lax.broadcasted_iota(jnp.int32, (32, BLK), 1)
    for r in range(1, 2 * SIDE):
        for cc in range(2):
            pltpu.make_async_remote_copy(
                src_ref=t_buf.at[r - 1, cc], dst_ref=e_buf.at[r - 1, cc], send_sem=send_sem.at[0],
                recv_sem=e_sem.at[r - 1, cc], device_id=at(x, y, z, other), device_id_type=MESH,
            ).wait_recv()
        one, two = e_buf[r - 1, 0], e_buf[r - 1, 1]
        upper = jnp.where(lane < 64, one, pltpu.roll(two, 64, 1))
        under = jnp.where(lane < 64, pltpu.roll(one, 64, 1), two)
        cols = pl.ds(pl.multiple_of(((pair + SIDE * SIDE - r) % (SIDE * SIDE)) * BLK, BLK), BLK)
        out_ref[0:32, cols] = first_ref[0:32, cols] - upper
        out_ref[32:64, cols] = first_ref[32:64, cols] - under

    for copy in sent:
        copy.wait_send()


def assemble(condensed, first_section):
    f32 = jnp.float32
    copies = 160

    def vmem(*shape):
        return pltpu.VMEM(shape, f32)

    s, r, w = SIDE, PIECE, WIDE
    return pl.pallas_call(
        assemble_kernel,
        out_shape=jax.ShapeDtypeStruct(first_section.shape, f32),
        in_specs=[pl.BlockSpec(memory_space=pl.ANY), pl.BlockSpec(memory_space=pltpu.VMEM)],
        out_specs=pl.BlockSpec(memory_space=pltpu.VMEM),
        scratch_shapes=[
            pltpu.VMEM(condensed.shape, condensed.dtype),
            pltpu.VMEM((2 * BLK, condensed.shape[0] * condensed.shape[1]), condensed.dtype),
            vmem(2, s, PARTS, s, s, r, w),
            vmem(s, 2, PARTS, 2, s, r, w),
            vmem(2, 2, s, r, w), vmem(s, 2, 2, r, w), vmem(s, 2, 2, r, w),
            vmem(s, s, r, w), vmem(s, s, r, w), vmem(s, s, r, w),
            vmem(s, s, r, w), vmem(s, s, r, w), vmem(s, s, r, w),
            vmem(PARTS, s, s, r, w), vmem(PARTS, 2, 2, r, w), vmem(PARTS, s, r, w), vmem(PARTS, s, r, w),
            vmem(PARTS, s, r, w), vmem(PARTS, 2, r // 2, w), vmem(PARTS, r, w), vmem(PARTS, r, w),
            vmem(4, PARTS, r, w), vmem(64, PARTS * w), vmem(7, 2, 32, BLK), vmem(7, 2, 32, BLK),
            pltpu.SemaphoreType.DMA((8,)),
            pltpu.SemaphoreType.DMA((copies,)),
            pltpu.SemaphoreType.DMA((copies,)),
            pltpu.SemaphoreType.DMA((7, 2)),
        ],
        compiler_params=pltpu.CompilerParams(
            collective_id=0, has_side_effects=True, vmem_limit_bytes=56 << 20
        ),
        name="assemble",
    )(condensed, first_section)


def body(inv_factor, border, block_rows, live_count, first_section):
    condensed = condense(live_count, block_rows, inv_factor, border)
    return condensed, assemble(condensed, first_section)


def solution(mesh):
    placed = (
        P(("grp", "dev"), None, None),
        P(("grp", "dev"), None, None),
        P(("grp", "dev")),
        P(("grp", "dev")),
        P("dev", None),
    )
    return jax.shard_map(
        body,
        mesh=mesh,
        in_specs=placed,
        out_specs=(P(("grp", "dev"), None, None), P("dev", None)),
        check_vma=False,
    )
```

time: 266 us -> 80.4 us (0.30)
  waiting for transfers between devices: 182 us -> 0 us
  Pallas kernels: 0 us -> 76.9 us
  blocking collectives: 27.9 us -> 0 us
  matrix products: 20.6 us -> 0 us
  between operations: 14.1 us -> 1.29 us
  local copies, waits for them, and re-layouts: 12.6 us -> 1.87 us
  other arithmetic: 3.28 us -> 0 us
    reduce_scatter x1 -> x0, waiting for transfers between devices: 182 us -> none  [body(): lax.psum_scatter(accumulate(condensed, count_own, lambda piece: column_pr...]
    pallas_call x0 -> x2, Pallas kernels: none -> 76.9 us  [the longest x1 66.7 us: assemble(): pl.pallas_call(assemble_kernel, out_shape=jax.ShapeDtypeStruct(first_sect...]
    all_to_all x1 -> x0, blocking collectives: 27.9 us -> none  [from_everyone(): lax.all_to_all(jnp.broadcast_to(value[None], (devices, *value.shape)), ax...]
    dot_general x2 -> x0, matrix products: 20.6 us -> none  [the longest x1 17 us: column_product(): lax.dot_general(columns, piece, (((0,), (0,)), ((), ())), preferred_eleme...]
    broadcast_in_dim x3 -> x0, local copies, waits for them, and re-layouts: 12.6 us -> none  [the longest x1 7.85 us: accumulate(): jnp.zeros(out_shape, jnp.float32)]
  transfers between devices with their start and end apart: 1 -> 0, of which waited for: 1 -> 0; matrix products, arithmetic and copies ran while one was open for 0% -> 0% of each run, Pallas kernels for 0% -> 0%
where the time goes in v1:
time: 80.4 us; the launch traced here: 80.1 us
  Pallas kernels  76.9 us (96%)
  local copies, waits for them, and re-layouts  1.87 us (2%)
  between operations  1.29 us (2%)
    pallas_call x1, Pallas kernels, assemble(): pl.pallas_call(assemble_kernel, out_shape=jax.ShapeDtypeStruct(first_sect...  66.7 us
    pallas_call x1, Pallas kernels, condense(): pl.pallas_call(condense_kernel, grid_spec=pltpu.PrefetchScalarGridSpec(nu...  10.2 us
    unnamed x1, local copies, waits for them, and re-layouts  1.87 us

profile of v1, /device:TPU:1, one launch (start us, length us, event | category | flops | bytes accessed | tf_op | source)
XLA Modules:
  0.0 80.1 jit_solution(6434602548008917644)
XLA Ops:
  1.3 10.2 %condense.1.cond_ref = bf16[4,384,2048]{2,1,0:T(8,128)(2,1)} custom-call(s32[1]{0:T(128)S(6)} %copy.8.live_ref, s32[4]{0:T(128)} %rows_ref.1, bf16[4,384,384]{2,1,0:T(8,128)(2,1)} %inv_ref.1, bf16[4,384,2048]{2,1,0:T(8,128)(2,1)} %border_ref.1), custom_call_target="tpu_custom_call" | custom-call | tf_op jit(solution)/shard_map/condense/pallas_call | solution.py:30
  11.5 66.7 %assemble.1 = f32[64,2048]{1,0:T(8,128)} custom-call(bf16[4,384,2048]{2,1,0:T(8,128)(2,1)} %condense.1.cond_ref, f32[64,2048]{1,0:T(8,128)} %first_ref.1), custom_call_target="tpu_custom_call" | custom-call | tf_op jit(solution)/shard_map/assemble/pallas_call | solution.py:324
  78.2 1.9 %copy.9 = f32[64,2048]{1,0:T(8,128)} copy(f32[64,2048]{1,0:T(8,128)} %assemble.1) | data formatting | bytes 1048576
